TPU v7x, 32 devices: a whole 2x2x4 slice. The times are simulated.
32 devices in a mesh: row: 4 (over y, core), col: 8 (over z, x).
Axes of the slice: x: 2, y: 2, z: 4, core: 2. Of those that a mesh axis runs over, the one named last changes fastest.
Arguments:
- rhs: bfloat16 [6144, 6144], P('row', 'col'), may hold values from -6 to 6
- basis_left: bfloat16 [6144, 6144], P('col', 'row'), may hold values from -1 to 1, as said below
- basis_right: bfloat16 [6144, 6144], P('row', 'col'), may hold values from -1 to 1, as said below
- eig_left: float32 [6144], P('row'), may hold values from 0.1 to 4
- eig_right: float32 [6144], P('col'), may hold values from 0.1 to 4
Outputs:
- solution: bfloat16 [6144, 6144], P('col', 'row')
Inputs may be any that keep to these rules, and one draw needn't show every extreme that they name: `basis_left`: an orthogonal matrix drawn uniformly, rounded to bfloat16. `basis_right`: an orthogonal matrix drawn uniformly, rounded to bfloat16.
All inputs are finite; a program needn't handle non-finite values.
Results may differ from a plain program's by a relative error of at most 0.0085.
Values may be sent and summed in bfloat16 or wider, within the bound.
A program may use at most 128 MiB of HBM per device.

v0:
```python
import jax
import jax.numpy as jnp
from jax import lax
from jax.sharding import PartitionSpec as P


def body(rhs, basis_left, basis_right, eig_left, eig_right):
    c_strip = lax.all_gather(rhs, "row", axis=0, tiled=True)
    left_all = lax.all_gather(basis_left, "col", axis=0, tiled=True)
    first = lax.dot_general(
        left_all, c_strip, (((0,), (0,)), ((), ())), preferred_element_type=jnp.float32
    )
    projected = first.astype(jnp.bfloat16)
    right_strip = lax.all_gather(basis_right, "row", axis=0, tiled=True)
    chosen = right_strip
    second = jnp.dot(
        lax.all_gather(projected, "col", axis=1, tiled=True),
        chosen,
        preferred_element_type=jnp.float32,
    )
    scaled = (second / (eig_left[:, None] + eig_right[None, :])).astype(jnp.bfloat16)
    chosen = left_all
    half = lax.psum_scatter(
        jnp.dot(chosen, scaled, preferred_element_type=jnp.float32),
        "row",
        scatter_dimension=0,
        tiled=True,
    ).astype(jnp.bfloat16)
    half_all = lax.all_gather(half, "row", axis=0, tiled=True)
    chosen = half_all
    return lax.psum_scatter(
        lax.dot_general(
            chosen, basis_right, (((1,), (1,)), ((), ())), preferred_element_type=jnp.float32
        ),
        "col",
        scatter_dimension=0,
        tiled=True,
    ).astype(jnp.bfloat16)


def solution(mesh):
    in_specs = (P("row", "col"), P("col", "row"), P("row", "col"), P("row"), P("col"))
    out_specs = P("col", "row")
    return jax.shard_map(body, mesh=mesh, in_specs=in_specs, out_specs=out_specs, check_vma=False)
```

profile of v0, /device:TPU:0, one launch (start us, length us, event | category | flops | bytes accessed | tf_op | source)
XLA Modules:
  0.0 1751.5 jit_solution(14869084896472922109)
XLA Ops:
  6.5 0.7 all-gather.8.cloned.1.call-update
  7.3 0.0 all-gather.6.cloned.1.call-start
  7.3 0.7 all-gather.6.cloned.1.call-update
  8.0 0.0 all-gather.12.cloned.1.call-start
  8.1 0.7 all-gather.12.cloned.1.call-update
  8.8 0.0 all-gather.10.cloned.1.call-start
  8.8 67.1 %all-gather.8.cloned.1.call-done = bf16[6144,768]{1,0:T(8,128)(2,1)} async-done(((bf16[1536,768]{1,0:T(8,128)(2,1)}), bf16[6144,768]{1,0:T(8,128)(2,1)}) %all-gather.8.cloned.1.call-update) | async-done | bytes 9437200 | tf_op jit(solution)/shard_map/all_gather | solution.py:8
  75.9 364.0 %all-gather.6.cloned.1.call-done = bf16[6144,1536]{1,0:T(8,128)(2,1)} async-done(((bf16[768,1536]{1,0:T(8,128)(2,1)}), bf16[6144,1536]{1,0:T(8,128)(2,1)}) %all-gather.6.cloned.1.call-update) | async-done | bytes 18874384 | tf_op jit(solution)/shard_map/all_gather | solution.py:9
  439.8 21.5 %convolution_convert_fusion = bf16[1536,768]{1,0:T(8,128)(2,1)} fusion(bf16[6144,1536]{1,0:T(8,128)(2,1)} %all-gather.6.cloned.1.call-done, bf16[6144,768]{1,0:T(8,128)(2,1)} %all-gather.8.cloned.1.call-done), kind=kOutput, calls=%fused_computation.2 | convolution fusion | flops 14496694272 | bytes 30670848 | tf_op jit(solution)/shard_map/dot_general | solution.py:10
  461.3 0.0 all-gather.10.cloned.1.call-update
  461.3 0.2 reduce-scatter.3.cloned.1.call-start
  461.5 44.1 %all-gather.12.cloned.1.call-done = bf16[6144,768]{1,0:T(8,128)(2,1)} async-done(((bf16[1536,768]{1,0:T(8,128)(2,1)}), bf16[6144,768]{1,0:T(8,128)(2,1)}) %all-gather.12.cloned.1.call-update) | async-done | bytes 9437200 | tf_op jit(solution)/shard_map/all_gather | solution.py:14
  505.6 363.8 %all-gather.10.cloned.1.call-done = bf16[1536,6144]{1,0:T(8,128)(2,1)} async-done(((bf16[1536,768]{1,0:T(8,128)(2,1)}), bf16[1536,6144]{1,0:T(8,128)(2,1)}) %all-gather.10.cloned.1.call-update) | async-done | bytes 18874384 | tf_op jit(solution)/shard_map/all_gather | solution.py:17
  869.4 20.6 %divide_convert_fusion = bf16[1536,768]{1,0:T(8,128)(2,1)S(1)} fusion(bf16[1536,6144]{1,0:T(8,128)(2,1)} %all-gather.10.cloned.1.call-done, bf16[6144,768]{1,0:T(8,128)(2,1)} %all-gather.12.cloned.1.call-done, f32[768]{0:T(1024)S(1)} %copy-done.2, f32[1536]{0:T(1024)S(1)} %copy-done.1), kind=kOutput, calls=%fused_computation.1 | convolution fusion | flops 14499053568 | bytes 30680064 | tf_op jit(solution)/shard_map/dot_general | solution.py:16
  890.1 20.7 %convolution_bitcast_fusion = f32[6144,768]{0,1:T(8,128)} fusion(bf16[1536,768]{1,0:T(8,128)(2,1)S(1)} %divide_convert_fusion, bf16[6144,1536]{1,0:T(8,128)(2,1)} %all-gather.6.cloned.1.call-done), kind=kOutput, calls=%fused_computation | convolution fusion | flops 14495514624 | bytes 40108032 | tf_op jit(solution)/shard_map/dot_general | solution.py:24
  910.8 0.0 all-gather.14.cloned.1.call-start
  910.9 137.8 %reduce-scatter.3.cloned.1.call-done = f32[1536,768]{0,1:T(8,128)} async-done(((f32[6144,768]{0,1:T(8,128)}), f32[1536,768]{0,1:T(8,128)}) %reduce-scatter.3.cloned.1.call-update) | async-done | bytes 4718608 | tf_op jit(solution)/shard_map/reduce_scatter | solution.py:23
  1048.7 4.0 convert_element_type.14
  1052.7 0.0 all-gather.14.cloned.1.call-update
  1052.7 0.3 reduce-scatter.5.cloned.1.call-start
  1053.0 64.1 %all-gather.14.cloned.1.call-done = bf16[6144,768]{0,1:T(8,128)(2,1)} async-done(((bf16[1536,768]{0,1:T(8,128)(2,1)}), bf16[6144,768]{0,1:T(8,128)(2,1)}) %all-gather.14.cloned.1.call-update) | async-done | bytes 9437200 | tf_op jit(solution)/shard_map/all_gather | solution.py:29
  1117.1 22.7 %fusion = f32[6144,1536]{1,0:T(8,128)} fusion(bf16[6144,768]{0,1:T(8,128)(2,1)} %all-gather.14.cloned.1.call-done, bf16[1536,768]{1,0:T(8,128)(2,1)S(1)} %copy-done), kind=kOutput, calls=%fused_computation.3 | convolution fusion | flops 14495514624 | bytes 49545216 | tf_op jit(solution)/shard_map/dot_general | solution.py:32
  1139.8 600.8 %reduce-scatter.5.cloned.1.call-done = f32[768,1536]{1,0:T(8,128)} async-done(((f32[6144,1536]{1,0:T(8,128)}), f32[768,1536]{1,0:T(8,128)}) %reduce-scatter.5.cloned.1.call-update) | async-done | bytes 4718608 | tf_op jit(solution)/shard_map/reduce_scatter | solution.py:31
  1740.6 4.0 convert_element_type.15
  (9 shorter events, 0.0 us)
Async XLA Ops:
  6.5 69.3 %all-gather.8.cloned.1.call-start = ((), (), s32[]{:S(2)}) async-start(), calls=%async_computation.3 | async-start | bytes 11796480 | tf_op jit(solution)/shard_map/all_gather | solution.py:8
  7.3 432.6 %all-gather.6.cloned.1.call-start = ((), (), s32[]{:S(2)}) async-start(), calls=%async_computation.2 | async-start | bytes 21233664 | tf_op jit(solution)/shard_map/all_gather | solution.py:9
  8.0 497.6 %all-gather.12.cloned.1.call-start = ((), (), s32[]{:S(2)}) async-start(), calls=%async_computation.5 | async-start | bytes 11796480 | tf_op jit(solution)/shard_map/all_gather | solution.py:14
  8.7 860.7 %copy-start.1 = (f32[1536]{0:T(1024)S(1)}, f32[1536]{0:T(1024)}, u32[]{:S(2)}) copy-start(f32[1536]{0:T(1024)} %param.8) | copy-start | bytes 18436
  8.8 860.7 %copy-start.2 = (f32[768]{0:T(1024)S(1)}, f32[768]{0:T(1024)}, u32[]{:S(2)}) copy-start(f32[768]{0:T(1024)} %param.9) | copy-start | bytes 9220
  8.8 860.7 %all-gather.10.cloned.1.call-start = ((), (), s32[]{:S(2)}) async-start(), calls=%async_computation.4 | async-start | bytes 21233664 | tf_op jit(solution)/shard_map/all_gather | solution.py:17
  461.3 587.4 %reduce-scatter.3.cloned.1.call-start = ((), (), s32[]{:S(2)}) async-start(), calls=%async_computation.6 | async-start | bytes 23592960 | tf_op jit(solution)/shard_map/reduce_scatter | solution.py:23
  910.8 206.3 %copy-start = (bf16[1536,768]{1,0:T(8,128)(2,1)S(1)}, bf16[1536,768]{1,0:T(8,128)(2,1)}, u32[]{:S(2)}) copy-start(bf16[1536,768]{1,0:T(8,128)(2,1)} %param.7) | copy-start | bytes 7077892
  910.8 206.3 %all-gather.14.cloned.1.call-start = ((), (), s32[]{:S(2)}) async-start(), calls=%async_computation.7 | async-start | bytes 11796480 | tf_op jit(solution)/shard_map/all_gather | solution.py:29
  1052.7 687.9 %reduce-scatter.5.cloned.1.call-start = ((), (), s32[]{:S(2)}) async-start(), calls=%async_computation.8 | async-start | bytes 42467328 | tf_op jit(solution)/shard_map/reduce_scatter | solution.py:31
Sparse Core Ops, SparseCore 0:
  8.9 66.9 all-gather.7
  77.4 362.3 all-gather.5
  441.4 64.1 all-gather.11
  507.0 362.3 all-gather.9
  910.9 137.7 reduce-scatter.2
  1052.8 64.2 all-gather.13
  1139.9 600.6 reduce-scatter.4
where the time goes:
time: 1750 us
  waiting for transfers between devices  1640 us (94%)
  matrix products  85.5 us (5%)
    reduce_scatter x1, waiting for transfers between devices, body(): lax.psum_scatter(lax.dot_general(chosen, basis_right, (((1,), (1,)), ((),...  601 us
    all_gather x1, waiting for transfers between devices, body(): left_all = lax.all_gather(basis_left, 'col', axis=0, tiled=True)  364 us
    all_gather x1, waiting for transfers between devices, body(): lax.all_gather(projected, 'col', axis=1, tiled=True)  364 us
    reduce_scatter x1, waiting for transfers between devices, body(): lax.psum_scatter(jnp.dot(chosen, scaled, preferred_element_type=jnp.float...  138 us
    all_gather x1, waiting for transfers between devices, body(): c_strip = lax.all_gather(rhs, 'row', axis=0, tiled=True)  67.1 us
    all_gather x1, waiting for transfers between devices, body(): half_all = lax.all_gather(half, 'row', axis=0, tiled=True)  64.1 us
    all_gather x1, waiting for transfers between devices, body(): right_strip = lax.all_gather(basis_right, 'row', axis=0, tiled=True)  44.1 us
  transfers between devices with their start and end apart: 7, of which 7 were waited for; matrix products, arithmetic and copies ran while one was open for 1% of the time, Pallas kernels for 0%

commit v1 on v0

--- a/solution.py
+++ b/solution.py
@@ -6,7 +6,15 @@
 
 def body(rhs, basis_left, basis_right, eig_left, eig_right):
     c_strip = lax.all_gather(rhs, "row", axis=0, tiled=True)
-    left_all = lax.all_gather(basis_left, "col", axis=0, tiled=True)
+    width = lax.axis_size("col")
+    step_out = basis_left
+    all_rows = [step_out]
+    block_last = sorted(((b, (b + 1) % width) for b in range(width)))
+    for h in tuple(range(1, width)):
+        step_out = lax.ppermute(step_out, "col", block_last)
+        all_rows.insert(0, step_out)
+    odd = jnp.concatenate(all_rows, axis=0)
+    left_all = jnp.roll(odd, (lax.axis_index("col") + 1) * basis_left.shape[0], axis=0)
     first = lax.dot_general(
         left_all, c_strip, (((0,), (0,)), ((), ())), preferred_element_type=jnp.float32
     )

time: 1750 us -> 1690 us (0.966)
  waiting for transfers between devices: 1640 us -> 1540 us
  local copies, waits for them, and re-layouts: 0.01 us -> 44.7 us
    ppermute x0 -> x7, waiting for transfers between devices: none -> 373 us  [body(): step_out = lax.ppermute(step_out, 'col', block_last)]
    all_gather x1 -> x0, waiting for transfers between devices: 364 us -> none  [body(): left_all = lax.all_gather(basis_left, 'col', axis=0, tiled=True)]
    all_gather x1, waiting for transfers between devices: 67.1 us -> 0.01 us  [body(): c_strip = lax.all_gather(rhs, 'row', axis=0, tiled=True)]
    all_gather x1, waiting for transfers between devices: 44.1 us -> 0.02 us  [body(): right_strip = lax.all_gather(basis_right, 'row', axis=0, tiled=True)]
    unnamed x6 -> x35, local copies, waits for them, and re-layouts: 0.01 us -> 43.1 us
  transfers between devices with their start and end apart: 7 -> 13, of which waited for: 7 -> 11; matrix products, arithmetic and copies ran while one was open for 1% -> 4% of each run, Pallas kernels for 0% -> 0%
where the time goes in v1:
time: 1690 us
  waiting for transfers between devices  1540 us (91%)
  matrix products  86 us (5%)
  local copies, waits for them, and re-layouts  44.7 us (3%)
    reduce_scatter x1, waiting for transfers between devices, body(): lax.psum_scatter(lax.dot_general(chosen, basis_right, (((1,), (1,)), ((),...  601 us
    ppermute x7, waiting for transfers between devices, body(): step_out = lax.ppermute(step_out, 'col', block_last)  373 us
    all_gather x1, waiting for transfers between devices, body(): lax.all_gather(projected, 'col', axis=1, tiled=True)  358 us
    reduce_scatter x1, waiting for transfers between devices, body(): lax.psum_scatter(jnp.dot(chosen, scaled, preferred_element_type=jnp.float...  138 us
    all_gather x1, waiting for transfers between devices, body(): half_all = lax.all_gather(half, 'row', axis=0, tiled=True)  64.1 us
    unnamed x35, local copies, waits for them, and re-layouts  43.1 us
  transfers between devices with their start and end apart: 13, of which 11 were waited for; matrix products, arithmetic and copies ran while one was open for 4% of the time, Pallas kernels for 0%

profile of v1, /device:TPU:0, one launch (start us, length us, event | category | flops | bytes accessed | tf_op | source)
XLA Modules:
  0.0 1691.3 jit_solution(4801309569217623508)
XLA Ops:
  10.3 54.5 %collective-permute-done = bf16[768,1536]{1,0:T(8,128)(2,1)S(1)} collective-permute-done((bf16[768,1536]{1,0:T(8,128)(2,1)}, bf16[768,1536]{1,0:T(8,128)(2,1)S(1)}, u32[]{:S(2)}, u32[]{:S(2)}) %collective-permute-start) | collective-permute-done | bytes 2359328 | tf_op jit(solution)/shard_map/ppermute | solution.py:14
  66.3 55.1 %collective-permute-done.1 = bf16[768,1536]{1,0:T(8,128)(2,1)S(1)} collective-permute-done((bf16[768,1536]{1,0:T(8,128)(2,1)S(1)}, bf16[768,1536]{1,0:T(8,128)(2,1)S(1)}, u32[]{:S(2)}, u32[]{:S(2)}) %collective-permute-start.1) | collective-permute-done | bytes 2359328 | tf_op jit(solution)/shard_map/ppermute | solution.py:14
  122.8 54.4 %collective-permute-done.2 = bf16[768,1536]{1,0:T(8,128)(2,1)} collective-permute-done((bf16[768,1536]{1,0:T(8,128)(2,1)S(1)}, bf16[768,1536]{1,0:T(8,128)(2,1)}, u32[]{:S(2)}, u32[]{:S(2)}) %collective-permute-start.2) | collective-permute-done | bytes 2359328 | tf_op jit(solution)/shard_map/ppermute | solution.py:14
  177.2 53.6 %collective-permute-done.3 = bf16[768,1536]{1,0:T(8,128)(2,1)} collective-permute-done((bf16[768,1536]{1,0:T(8,128)(2,1)}, bf16[768,1536]{1,0:T(8,128)(2,1)}, u32[]{:S(2)}, u32[]{:S(2)}) %collective-permute-start.3) | collective-permute-done | bytes 2359328 | tf_op jit(solution)/shard_map/ppermute | solution.py:14
  230.9 52.7 %collective-permute-done.4 = bf16[768,1536]{1,0:T(8,128)(2,1)S(1)} collective-permute-done((bf16[768,1536]{1,0:T(8,128)(2,1)}, bf16[768,1536]{1,0:T(8,128)(2,1)S(1)}, u32[]{:S(2)}, u32[]{:S(2)}) %collective-permute-start.4) | collective-permute-done | bytes 2359328 | tf_op jit(solution)/shard_map/ppermute | solution.py:14
  285.0 51.8 %collective-permute-done.5 = bf16[768,1536]{1,0:T(8,128)(2,1)} collective-permute-done((bf16[768,1536]{1,0:T(8,128)(2,1)S(1)}, bf16[768,1536]{1,0:T(8,128)(2,1)}, u32[]{:S(2)}, u32[]{:S(2)}) %collective-permute-start.5) | collective-permute-done | bytes 2359328 | tf_op jit(solution)/shard_map/ppermute | solution.py:14
  336.8 51.1 %collective-permute-done.6 = bf16[768,1536]{1,0:T(8,128)(2,1)} collective-permute-done((bf16[768,1536]{1,0:T(8,128)(2,1)}, bf16[768,1536]{1,0:T(8,128)(2,1)}, u32[]{:S(2)}, u32[]{:S(2)}) %collective-permute-start.6) | collective-permute-done | bytes 2359328 | tf_op jit(solution)/shard_map/ppermute | solution.py:14
  387.9 3.2 constant_dynamic-update-slice_fusion.15
  391.2 3.3 constant_dynamic-update-slice_fusion.14
  394.5 3.4 constant_dynamic-update-slice_fusion.13
  397.9 3.3 constant_dynamic-update-slice_fusion.12
  409.1 3.2 constant_dynamic-update-slice_fusion.7
  412.3 3.3 constant_dynamic-update-slice_fusion.6
  420.4 3.3 constant_dynamic-update-slice_fusion.3
  428.4 21.5 %fusion.4 = bf16[1536,768]{1,0:T(8,128)(2,1)} fusion(bf16[6144,768]{1,0:T(8,128)(2,1)} %all-gather.5.cloned.1.call-done, bf16[12288,1536]{1,0:T(8,128)(2,1)} %constant_dynamic-update-slice_fusion, s32[]{:T(128)S(6)} %select_n.14), kind=kOutput, calls=%fused_computation.5 | convolution fusion | flops 14496694272 | bytes 30670852 | tf_op jit(solution)/shard_map/dot_general | solution.py:18
  450.2 358.4 %all-gather.7.cloned.1.call-done = bf16[1536,6144]{1,0:T(8,128)(2,1)} async-done(((bf16[1536,768]{1,0:T(8,128)(2,1)}), bf16[1536,6144]{1,0:T(8,128)(2,1)}) %all-gather.7.cloned.1.call-update) | async-done | bytes 18874384 | tf_op jit(solution)/shard_map/all_gather | solution.py:25
  808.7 20.6 %divide_convert_fusion = bf16[1536,768]{1,0:T(8,128)(2,1)S(1)} fusion(bf16[1536,6144]{1,0:T(8,128)(2,1)} %all-gather.7.cloned.1.call-done, bf16[6144,768]{1,0:T(8,128)(2,1)} %all-gather.9.cloned.1.call-done, f32[768]{0:T(1024)S(1)} %copy-done.9, f32[1536]{0:T(1024)S(1)} %copy-done.8), kind=kOutput, calls=%fused_computation.4 | convolution fusion | flops 14499053568 | bytes 30680064 | tf_op jit(solution)/shard_map/dot_general | solution.py:24
  829.3 21.3 %fusion = f32[6144,768]{1,0:T(8,128)} fusion(bf16[1536,768]{1,0:T(8,128)(2,1)S(1)} %divide_convert_fusion, bf16[12288,1536]{1,0:T(8,128)(2,1)} %constant_dynamic-update-slice_fusion, s32[]{:T(128)S(6)} %select_n.14), kind=kOutput, calls=%fused_computation | convolution fusion | flops 14495514624 | bytes 40108036 | tf_op jit(solution)/shard_map/dot_general | solution.py:32
  850.7 137.9 %reduce-scatter.3.cloned.1.call-done = f32[1536,768]{1,0:T(8,128)} async-done(((f32[6144,768]{1,0:T(8,128)}), f32[1536,768]{1,0:T(8,128)}) %reduce-scatter.3.cloned.1.call-update) | async-done | bytes 4718608 | tf_op jit(solution)/shard_map/reduce_scatter | solution.py:31
  988.6 4.0 convert_element_type.14
  992.8 64.1 %all-gather.11.cloned.1.call-done = bf16[6144,768]{1,0:T(8,128)(2,1)} async-done(((bf16[1536,768]{1,0:T(8,128)(2,1)}), bf16[6144,768]{1,0:T(8,128)(2,1)}) %all-gather.11.cloned.1.call-update) | async-done | bytes 9437200 | tf_op jit(solution)/shard_map/all_gather | solution.py:37
  1056.9 22.6 %fusion.9 = f32[6144,1536]{1,0:T(8,128)} fusion(bf16[6144,768]{1,0:T(8,128)(2,1)} %all-gather.11.cloned.1.call-done, bf16[1536,768]{1,0:T(8,128)(2,1)S(1)} %copy-done.7), kind=kOutput, calls=%fused_computation.24 | convolution fusion | flops 14495514624 | bytes 49545216 | tf_op jit(solution)/shard_map/dot_general | solution.py:40
  1079.5 600.9 %reduce-scatter.5.cloned.1.call-done = f32[768,1536]{1,0:T(8,128)} async-done(((f32[6144,1536]{1,0:T(8,128)}), f32[768,1536]{1,0:T(8,128)}) %reduce-scatter.5.cloned.1.call-update) | async-done | bytes 4718608 | tf_op jit(solution)/shard_map/reduce_scatter | solution.py:39
  1680.5 4.0 convert_element_type.15
  (50 shorter events, 26.2 us)
Async XLA Ops:
  6.5 401.0 %copy-start = (bf16[768,1536]{1,0:T(8,128)(2,1)S(1)}, bf16[768,1536]{1,0:T(8,128)(2,1)}, u32[]{:S(2)}) copy-start(bf16[768,1536]{1,0:T(8,128)(2,1)} %param.6) | copy-start | bytes 7077892
  6.5 421.9 %all-gather.5.cloned.1.call-start = ((), (), s32[]{:S(2)}) async-start(), calls=%async_computation.2 | async-start | bytes 11796480 | tf_op jit(solution)/shard_map/all_gather | solution.py:8
  7.3 443.0 %all-gather.9.cloned.1.call-start = ((), (), s32[]{:S(2)}) async-start(), calls=%async_computation.4 | async-start | bytes 11796480 | tf_op jit(solution)/shard_map/all_gather | solution.py:22
  7.3 57.5 %collective-permute-start = (bf16[768,1536]{1,0:T(8,128)(2,1)}, bf16[768,1536]{1,0:T(8,128)(2,1)S(1)}, u32[]{:S(2)}, u32[]{:S(2)}) collective-permute-start(bf16[768,1536]{1,0:T(8,128)(2,1)} %param.6), channel_id=1, source_target_pairs={{0,1},{1,2},{2,3},{3,4},{4,5},{5,6},{6,7},{7,0},{8,9},{9,10},{10,1... | collective-permute-start | bytes 7077896 | tf_op jit(solution)/shard_map/ppermute | solution.py:14
  64.8 1.4 copy-start.1
  66.3 55.1 %collective-permute-start.1 = (bf16[768,1536]{1,0:T(8,128)(2,1)S(1)}, bf16[768,1536]{1,0:T(8,128)(2,1)S(1)}, u32[]{:S(2)}, u32[]{:S(2)}) collective-permute-start(bf16[768,1536]{1,0:T(8,128)(2,1)S(1)} %collective-permute-done), channel_id=1, source_target_pairs={{0,1},{1,2},{2,3},{3,4},{4,5},{5,6},{6,7},{7,0},{8,9},{9,10},{10,1... | collective-permute-start | bytes 7077896 | tf_op jit(solution)/shard_map/ppermute | solution.py:14
  121.4 1.4 copy-start.3
  122.8 54.4 %collective-permute-start.2 = (bf16[768,1536]{1,0:T(8,128)(2,1)S(1)}, bf16[768,1536]{1,0:T(8,128)(2,1)}, u32[]{:S(2)}, u32[]{:S(2)}) collective-permute-start(bf16[768,1536]{1,0:T(8,128)(2,1)S(1)} %collective-permute-done.1), channel_id=1, source_target_pairs={{0,1},{1,2},{2,3},{3,4},{4,5},{5,6},{6,7},{7,0},{8,9},{9,10},{10,1... | collective-permute-start | bytes 7077896 | tf_op jit(solution)/shard_map/ppermute | solution.py:14
  177.1 53.7 %collective-permute-start.3 = (bf16[768,1536]{1,0:T(8,128)(2,1)}, bf16[768,1536]{1,0:T(8,128)(2,1)}, u32[]{:S(2)}, u32[]{:S(2)}) collective-permute-start(bf16[768,1536]{1,0:T(8,128)(2,1)} %collective-permute-done.2), channel_id=1, source_target_pairs={{0,1},{1,2},{2,3},{3,4},{4,5},{5,6},{6,7},{7,0},{8,9},{9,10},{10,1... | collective-permute-start | bytes 7077896 | tf_op jit(solution)/shard_map/ppermute | solution.py:14
  177.2 631.5 %all-gather.7.cloned.1.call-start = ((), (), s32[]{:S(2)}) async-start(), calls=%async_computation.3 | async-start | bytes 21233664 | tf_op jit(solution)/shard_map/all_gather | solution.py:25
  230.8 52.8 %collective-permute-start.4 = (bf16[768,1536]{1,0:T(8,128)(2,1)}, bf16[768,1536]{1,0:T(8,128)(2,1)S(1)}, u32[]{:S(2)}, u32[]{:S(2)}) collective-permute-start(bf16[768,1536]{1,0:T(8,128)(2,1)} %collective-permute-done.3), channel_id=1, source_target_pairs={{0,1},{1,2},{2,3},{3,4},{4,5},{5,6},{6,7},{7,0},{8,9},{9,10},{10,1... | collective-permute-start | bytes 7077896 | tf_op jit(solution)/shard_map/ppermute | solution.py:14
  283.6 1.4 copy-start.5
  285.0 51.8 %collective-permute-start.5 = (bf16[768,1536]{1,0:T(8,128)(2,1)S(1)}, bf16[768,1536]{1,0:T(8,128)(2,1)}, u32[]{:S(2)}, u32[]{:S(2)}) collective-permute-start(bf16[768,1536]{1,0:T(8,128)(2,1)S(1)} %collective-permute-done.4), channel_id=1, source_target_pairs={{0,1},{1,2},{2,3},{3,4},{4,5},{5,6},{6,7},{7,0},{8,9},{9,10},{10,1... | collective-permute-start | bytes 7077896 | tf_op jit(solution)/shard_map/ppermute | solution.py:14
  336.8 51.1 %collective-permute-start.6 = (bf16[768,1536]{1,0:T(8,128)(2,1)}, bf16[768,1536]{1,0:T(8,128)(2,1)}, u32[]{:S(2)}, u32[]{:S(2)}) collective-permute-start(bf16[768,1536]{1,0:T(8,128)(2,1)} %collective-permute-done.5), channel_id=1, source_target_pairs={{0,1},{1,2},{2,3},{3,4},{4,5},{5,6},{6,7},{7,0},{8,9},{9,10},{10,1... | collective-permute-start | bytes 7077896 | tf_op jit(solution)/shard_map/ppermute | solution.py:14
  336.8 67.6 %copy-start.4 = (bf16[768,1536]{1,0:T(8,128)(2,1)S(1)}, bf16[768,1536]{1,0:T(8,128)(2,1)}, u32[]{:S(2)}) copy-start(bf16[768,1536]{1,0:T(8,128)(2,1)} %copy-done.3) | copy-start | bytes 7077892
  336.8 69.2 %copy-start.2 = (bf16[768,1536]{1,0:T(8,128)(2,1)S(1)}, bf16[768,1536]{1,0:T(8,128)(2,1)}, u32[]{:S(2)}) copy-start(bf16[768,1536]{1,0:T(8,128)(2,1)} %copy-done.1) | copy-start | bytes 7077892
  394.5 21.1 %copy-start.6 = (bf16[768,1536]{1,0:T(8,128)(2,1)S(1)}, bf16[768,1536]{1,0:T(8,128)(2,1)}, u32[]{:S(2)}) copy-start(bf16[768,1536]{1,0:T(8,128)(2,1)} %copy-done.5) | copy-start | bytes 7077892
  428.4 380.3 %copy-start.8 = (f32[1536]{0:T(1024)S(1)}, f32[1536]{0:T(1024)}, u32[]{:S(2)}) copy-start(f32[1536]{0:T(1024)} %param.8) | copy-start | bytes 18436
  428.4 380.3 %copy-start.9 = (f32[768]{0:T(1024)S(1)}, f32[768]{0:T(1024)}, u32[]{:S(2)}) copy-start(f32[768]{0:T(1024)} %param.9) | copy-start | bytes 9220
  450.0 538.6 %reduce-scatter.3.cloned.1.call-start = ((), (), s32[]{:S(2)}) async-start(), calls=%async_computation.5 | async-start | bytes 23592960 | tf_op jit(solution)/shard_map/reduce_scatter | solution.py:31
  850.6 206.4 %copy-start.7 = (bf16[1536,768]{1,0:T(8,128)(2,1)S(1)}, bf16[1536,768]{1,0:T(8,128)(2,1)}, u32[]{:S(2)}) copy-start(bf16[1536,768]{1,0:T(8,128)(2,1)} %param.7) | copy-start | bytes 7077892
  850.6 206.3 %all-gather.11.cloned.1.call-start = ((), (), s32[]{:S(2)}) async-start(), calls=%async_computation.6 | async-start | bytes 11796480 | tf_op jit(solution)/shard_map/all_gather | solution.py:37
  992.5 687.9 %reduce-scatter.5.cloned.1.call-start = ((), (), s32[]{:S(2)}) async-start(), calls=%async_computation.7 | async-start | bytes 42467328 | tf_op jit(solution)/shard_map/reduce_scatter | solution.py:39
Sparse Core Ops, SparseCore 0:
  8.9 66.9 all-gather.4
  177.3 65.2 all-gather.8
  450.1 358.5 all-gather.6
  850.7 137.7 reduce-scatter.2
  992.7 64.2 all-gather.10
  1079.6 600.7 reduce-scatter.4
